TPU v7x, 512 devices: a whole 4x4x16 slice. The times are simulated.
512 devices in a mesh: dp: 32 (over y, z_lo), mp: 16 (over x, z_hi, core).
Axes of the slice: x: 4, y: 4, z: 16 (z_hi: 2, z_lo: 8; z = z_hi * 8 + z_lo), core: 2. Of those that a mesh axis runs over, the one named last changes fastest.
Arguments:
- logits: bfloat16 [4096, 65536], P('dp', 'mp'), may hold values from -72 to 240
- targets: int32 [4096], P('dp'), may hold values from 0 to 65535
- resp_mask: int32 [4096], P('dp'), may hold values from 0 to 1, as said below
- rewards: int32 [32], P('dp'), may hold values from 0 to 10
- groups: int32 [32], P('dp'), may hold values from 0 to 7, as said below
- unit_grad: bfloat16 [4096, 8192], P(('dp', 'mp')), may hold values from -192 to 192
- mix: bfloat16 [4096, 8192], P('dp', 'mp'), may hold values from -6 to 6
- w_out: bfloat16 [8192, 8192], P('mp', 'dp'), may hold values from -0.0625 to 0.0625
Outputs:
- token_logprob: float32 [4096], P('dp')
- policy_loss: float32 [], replicated
- grad_mix: bfloat16 [4096, 8192], P('dp', 'mp')
- grad_w_out: bfloat16 [8192, 8192], P('mp', 'dp')
Inputs may be any that keep to these rules, and one draw needn't show every extreme that they name: `resp_mask`: in each sample the response mask is a run of ones followed by zeros, with at least 32 ones. `groups`: each prompt id names exactly 4 samples.
All inputs are finite; a program needn't handle non-finite values.
Results may differ from a plain program's by a relative error of at most 0.005.
Values may be sent and summed in bfloat16 or wider, within the bound.
A program may use at most 64 MiB of HBM per device.

v0:
```python
import jax
import jax.numpy as jnp
from jax import lax
from jax.sharding import Mesh
from jax.sharding import PartitionSpec as P

K = 4
DP = ("dp_0", "dp_1")
DP_MP = ("dp_0", "dp_1", "mp")


def from_everyone(shard, axis):
    count = lax.axis_size(axis)
    return lax.all_to_all(
        jnp.broadcast_to(shard[None], (count, *shard.shape)), axis, 0, 0, tiled=True
    )


def collected_together(shard, axis):
    leaves = jax.tree.leaves(shard)
    sequence = sorted(range(len(leaves)), key=lambda k: -leaves[k].size)
    width = (1, *leaves[sequence[0]].shape)[-1]
    lines = [
        jnp.pad(leaves[k].reshape(-1), (0, -leaves[k].size % width)).reshape(-1, width)
        for k in sequence
    ]
    both, at, found = (from_everyone(jnp.concatenate(lines), axis), 0, {})
    for k, line in zip(sequence, lines):
        piece = both[:, at : at + len(line)].reshape(len(both), -1)
        found[k] = piece[:, : leaves[k].size].reshape(-1, *leaves[k].shape)
        at += len(line)
    numbers = iter(range(len(leaves)))
    return jax.tree.map(lambda _: found[next(numbers)], shard)


def joined_by_halves(pieces, combine):
    while len(jax.tree.leaves(pieces)[0]) > 1:
        pieces = jax.vmap(combine)(
            *(jax.tree.map(lambda part: part[side::2], pieces) for side in (0, 1))
        )
    return jax.tree.map(lambda part: part[0], pieces)


def merged(shard, axis, combine):
    pieces = collected_together(shard, axis)
    return joined_by_halves(pieces, combine)


def of_everyone(shard, axis):
    everything = from_everyone(shard, axis)
    return jnp.sum(everything, axis=0)


def packed_total(arrays, axis):
    vector, at, gathered = (jnp.concatenate([a.reshape(-1) for a in arrays]), 0, [])
    total = of_everyone(vector, axis)
    for a in arrays:
        gathered.append(total[at : at + a.size].reshape(a.shape))
        at += a.size
    return tuple(gathered)


def whole_of(shard, axes, dim):
    for axis in reversed(axes):
        shard = lax.all_gather(shard, axis, axis=dim, tiled=True)
    return shard


def merge_stats(first, second):
    highest = jnp.maximum(first[0], second[0])
    summed = first[1] * jnp.exp(first[0] - highest) + second[1] * jnp.exp(second[0] - highest)
    return (highest, summed, first[2] + second[2])


def shards(logits, targets, resp_mask, rewards, groups, unit_grad, mix, w_out):
    tok_rows, vocab_dev = logits.shape
    mp_lane = lax.axis_index("mp")
    local_target = targets - mp_lane * vocab_dev
    present = (local_target >= 0) & (local_target < vocab_dev)
    picked = jnp.take_along_axis(logits, jnp.clip(local_target, 0, vocab_dev - 1)[:, None], axis=1)[
        :, 0
    ]
    picked = jnp.where(present, picked.astype(jnp.float32), 0.0)
    local_max = jnp.max(logits, axis=1).astype(jnp.float32)
    local_sum = jnp.sum(jnp.exp(logits.astype(jnp.float32) - local_max[:, None]), axis=1)
    highest, summed, target_logit = merged((local_max, local_sum, picked), "mp", merge_stats)
    logprob = target_logit - (highest + jnp.log(summed))
    mask_float = resp_mask.astype(jnp.float32)
    local_count = jnp.sum(mask_float)
    reward_float = rewards.astype(jnp.float32)
    prompt_slots = jnp.arange(lax.axis_size(DP) // K, dtype=jnp.int32)
    own_slot = (prompt_slots == groups[0]).astype(jnp.float32)
    group_total, token_count = packed_total((own_slot * reward_float[0], local_count), DP)
    own_total = jnp.sum(own_slot * group_total)
    advantage = reward_float[0] - (own_total - reward_float[0]) / (K - 1)
    weight = advantage * mask_float / token_count
    policy_loss = of_everyone(-jnp.sum(weight * logprob), DP)
    sub_rows = unit_grad.shape[0]
    part_weight = lax.dynamic_slice_in_dim(weight, mp_lane * sub_rows, sub_rows)
    grad_local = (-part_weight[:, None] * unit_grad.astype(jnp.float32)).astype(jnp.bfloat16)
    grad_group = lax.all_gather(grad_local, "mp", axis=0, tiled=True)
    grad_mix = lax.dot_general(
        grad_group,
        whole_of(w_out, DP, 1),
        (((1,), (1,)), ((), ())),
        preferred_element_type=jnp.float32,
    ).astype(jnp.bfloat16)
    grad_every = lax.all_to_all(grad_group, DP, split_axis=1, concat_axis=0, tiled=True)
    grad_w_out = lax.dot_general(
        lax.all_gather(mix, DP, axis=0, tiled=True),
        grad_every,
        (((0,), (0,)), ((), ())),
        preferred_element_type=jnp.float32,
    ).astype(jnp.bfloat16)
    return (logprob, policy_loss, grad_mix, grad_w_out)


def solution(mesh):
    finer = Mesh(mesh.devices.reshape(4, 8, mesh.shape["mp"]), ("dp_0", "dp_1", "mp"))
    in_specs = (P(DP, "mp"), P(DP), P(DP), P(DP), P(DP), P(DP_MP, None), P(DP, "mp"), P("mp", DP))
    out_specs = (P(DP), P(), P(DP, "mp"), P("mp", DP))
    return jax.shard_map(
        shards, mesh=finer, in_specs=in_specs, out_specs=out_specs, check_vma=False
    )
```

profile of v0, /device:TPU:1, one launch (start us, length us, event | category | flops | bytes accessed | tf_op | source)
XLA Modules:
  0.0 563.2 jit_solution(692002191340332963)
XLA Ops:
  7.2 0.0 copy-start.2
  7.2 0.0 copy-start.3
  7.2 0.0 copy-start.1
  7.2 1.3 convert_reduce_fusion
  9.8 0.7 pad_maximum_fusion.1
  10.5 0.6 broadcast_in_dim.17
  11.2 16.1 %all-to-all-start.1 = ((f32[32,1,9]{2,1,0:T(1,128)}), f32[32,1,9]{2,1,0:T(1,128)S(1)}, u32[]{:S(2)}, u32[]{:S(2)}) async-start(f32[32,1,9]{2,1,0:T(1,128)} %broadcast_in_dim.17), calls=%async_computation.1 | async-start | bytes 32768 | tf_op jit(solution)/shard_map/all_to_all | solution.py:14
  27.2 0.0 all-gather.7.cloned.1.call-start
  27.3 0.7 all-gather.7.cloned.1.call-update
  28.0 0.7 fusion.5
  28.7 2.3 gather_fusion
  31.0 1.4 reduce_max.9
  32.5 1.7 exponential_reduce_fusion
  34.2 0.0 copy-done.3
  34.2 4.3 all-to-all-done.1
  38.5 0.6 broadcast_in_dim.16
  39.2 12.2 %all-to-all-start = ((f32[16,3,128]{2,1,0:T(4,128)}), f32[16,3,128]{2,1,0:T(4,128)S(1)}, u32[]{:S(2)}, u32[]{:S(2)}) async-start(f32[16,3,128]{2,1,0:T(4,128)} %broadcast_in_dim.16), calls=%async_computation | async-start | bytes 65536 | tf_op jit(solution)/shard_map/all_to_all | solution.py:14
  51.3 0.0 all-gather.5.cloned.1.call-start
  51.4 0.1 reduce_sum.56
  51.4 0.6 slice.121
  52.0 0.6 fusion.1
  53.3 12.7 %all-to-all-done = f32[16,3,128]{2,1,0:T(4,128)S(1)} async-done(((f32[16,3,128]{2,1,0:T(4,128)}), f32[16,3,128]{2,1,0:T(4,128)S(1)}, u32[]{:S(2)}, u32[]{:S(2)}) %all-to-all-start) | async-done | bytes 24608 | tf_op jit(solution)/shard_map/all_to_all | solution.py:14
  66.4 0.0 copy-done.2
  66.4 1.8 multiply_reduce_fusion
  68.2 0.1 dynamic-slice_negate_fusion
  68.2 0.0 copy-done.1
  68.2 0.7 multiply_convert_fusion
  69.0 0.0 all-gather.5.cloned.1.call-update
  69.0 0.0 all-gather.11.cloned.1.call-start
  69.1 0.7 all-gather.11.cloned.1.call-update
  69.8 0.0 all-gather.9.cloned.1.call-start
  69.8 30.2 %all-gather.7.cloned.1.call-done = bf16[512,2048]{1,0:T(8,128)(2,1)} async-done(((bf16[512,256]{1,0:T(8,128)(2,1)}), bf16[512,2048]{1,0:T(8,128)(2,1)}) %all-gather.7.cloned.1.call-update) | async-done | bytes 2097168 | tf_op jit(solution)/shard_map/all_gather | solution.py:65
  100.0 0.0 all-gather.9.cloned.1.call-update
  100.6 0.6 broadcast_in_dim.18
  101.3 9.8 %all-to-all-start.2 = ((f32[32,1,1]{2,1,0:T(1,128)}), f32[32,1,1]{2,1,0:T(1,128)S(1)}, u32[]{:S(2)}, u32[]{:S(2)}) async-start(f32[32,1,1]{2,1,0:T(1,128)} %broadcast_in_dim.18), calls=%async_computation.2 | async-start | bytes 32768 | tf_op jit(solution)/shard_map/all_to_all | solution.py:14
  111.1 83.4 %all-gather.5.cloned.1.call-done = bf16[128,8192]{1,0:T(8,128)(2,1)} async-done(((bf16[8,8192]{1,0:T(8,128)(2,1)}), bf16[128,8192]{1,0:T(8,128)(2,1)}) %all-gather.5.cloned.1.call-update) | async-done | bytes 2097168 | tf_op jit(solution)/shard_map/all_gather | solution.py:101
  194.4 4.1 copy.39
  198.5 0.0 all-to-all-done.2
  198.5 4.8 all-to-all-start.3
  203.3 0.6 reduce_sum.59
  204.0 125.4 %all-to-all-done.3 = bf16[128,32,256]{0,2,1:T(8,128)(2,1)S(1)} async-done(((bf16[128,32,256]{0,2,1:T(8,128)(2,1)}), bf16[128,32,256]{0,2,1:T(8,128)(2,1)S(1)}, u32[]{:S(2)}, u32[]{:S(2)}) %all-to-all-start.3) | async-done | bytes 2097184 | tf_op jit(solution)/shard_map/all_to_all | solution.py:108
  329.4 2.9 copy.40
  332.3 111.9 %all-gather.11.cloned.1.call-done = bf16[4096,512]{1,0:T(8,128)(2,1)} async-done(((bf16[128,512]{1,0:T(8,128)(2,1)}), bf16[4096,512]{1,0:T(8,128)(2,1)}) %all-gather.11.cloned.1.call-update) | async-done | bytes 4194320 | tf_op jit(solution)/shard_map/all_gather | solution.py:110
  444.2 4.2 fusion
  448.5 0.8 copy.41
  449.3 100.4 %all-gather.9.cloned.1.call-done = bf16[512,8192]{1,0:T(8,128)(2,1)} async-done(((bf16[512,2048]{1,0:T(8,128)(2,1)}), bf16[512,8192]{1,0:T(8,128)(2,1)}) %all-gather.9.cloned.1.call-update) | async-done | bytes 8388624 | tf_op jit(solution)/shard_map/all_gather | solution.py:65
  549.7 0.0 copy-done
  549.7 7.0 %convolution_convert_fusion.1 = bf16[128,512]{1,0:T(8,128)(2,1)} fusion(bf16[128,8192]{1,0:T(8,128)(2,1)S(1)} %copy-done, bf16[512,8192]{1,0:T(8,128)(2,1)} %all-gather.9.cloned.1.call-done), kind=kOutput, calls=%fused_computation.4 | convolution fusion | flops 1073807360 | bytes 10616832 | tf_op jit(solution)/shard_map/dot_general | solution.py:102
  (33 shorter events, 0.5 us)
Async XLA Ops:
  7.2 59.2 %copy-start.2 = (s32[128]{0:T(128)S(1)}, s32[128]{0:T(128)}, u32[]{:S(2)}) copy-start(s32[128]{0:T(128)} %param.10) | copy-start | bytes 1540
  7.2 27.0 %copy-start.3 = (s32[128]{0:T(128)S(1)}, s32[128]{0:T(128)}, u32[]{:S(2)}) copy-start(s32[128]{0:T(128)} %param.9) | copy-start | bytes 1540
  7.2 61.1 %copy-start.1 = (bf16[8,8192]{1,0:T(8,128)(2,1)S(1)}, bf16[8,8192]{1,0:T(8,128)(2,1)}, u32[]{:S(2)}) copy-start(bf16[8,8192]{1,0:T(8,128)(2,1)} %param.13) | copy-start | bytes 393220
  11.2 27.4 %all-to-all-start.1 = ((f32[32,1,9]{2,1,0:T(1,128)}), f32[32,1,9]{2,1,0:T(1,128)S(1)}, u32[]{:S(2)}, u32[]{:S(2)}) async-start(f32[32,1,9]{2,1,0:T(1,128)} %broadcast_in_dim.17), calls=%async_computation.1 | async-start | bytes 32768 | tf_op jit(solution)/shard_map/all_to_all | solution.py:14
  27.2 72.7 %all-gather.7.cloned.1.call-start = ((), (), s32[]{:S(2)}) async-start(), calls=%async_computation.5 | async-start | bytes 2359296 | tf_op jit(solution)/shard_map/all_gather | solution.py:65
  39.2 26.8 %all-to-all-start = ((f32[16,3,128]{2,1,0:T(4,128)}), f32[16,3,128]{2,1,0:T(4,128)S(1)}, u32[]{:S(2)}, u32[]{:S(2)}) async-start(f32[16,3,128]{2,1,0:T(4,128)} %broadcast_in_dim.16), calls=%async_computation | async-start | bytes 65536 | tf_op jit(solution)/shard_map/all_to_all | solution.py:14
  51.3 143.1 %all-gather.5.cloned.1.call-start = ((), (), s32[]{:S(2)}) async-start(), calls=%async_computation.4 | async-start | bytes 2228224 | tf_op jit(solution)/shard_map/all_gather | solution.py:101
  69.0 375.2 %all-gather.11.cloned.1.call-start = ((), (), s32[]{:S(2)}) async-start(), calls=%async_computation.7 | async-start | bytes 4325376 | tf_op jit(solution)/shard_map/all_gather | solution.py:110
  69.8 479.9 %all-gather.9.cloned.1.call-start = ((), (), s32[]{:S(2)}) async-start(), calls=%async_computation.6 | async-start | bytes 10485760 | tf_op jit(solution)/shard_map/all_gather | solution.py:65
  101.3 97.2 %all-to-all-start.2 = ((f32[32,1,1]{2,1,0:T(1,128)}), f32[32,1,1]{2,1,0:T(1,128)S(1)}, u32[]{:S(2)}, u32[]{:S(2)}) async-start(f32[32,1,1]{2,1,0:T(1,128)} %broadcast_in_dim.18), calls=%async_computation.2 | async-start | bytes 32768 | tf_op jit(solution)/shard_map/all_to_all | solution.py:14
  198.5 130.9 %all-to-all-start.3 = ((bf16[128,32,256]{0,2,1:T(8,128)(2,1)}), bf16[128,32,256]{0,2,1:T(8,128)(2,1)S(1)}, u32[]{:S(2)}, u32[]{:S(2)}) async-start(bf16[128,32,256]{0,2,1:T(8,128)(2,1)} %bitcast.14), calls=%async_computation.3 | async-start | bytes 4194304 | tf_op jit(solution)/shard_map/all_to_all | solution.py:108
  444.2 105.5 %copy-start = (bf16[128,8192]{1,0:T(8,128)(2,1)S(1)}, bf16[128,8192]{1,0:T(8,128)(2,1)}, u32[]{:S(2)}) copy-start(bf16[128,8192]{1,0:T(8,128)(2,1)} %all-gather.5.cloned.1.call-done) | copy-start | bytes 6291460
Sparse Core Ops, SparseCore 0:
  30.1 69.8 all-gather.6
  103.8 90.5 all-gather.4
  196.5 247.6 all-gather.10
  446.2 103.4 all-gather.8
where the time goes:
time: 564 us; the launch traced here: 563 us
  waiting for transfers between devices  470 us (83%)
  starting transfers between devices  43 us (8%)
  between operations  16.5 us (3%)
  local copies, waits for them, and re-layouts  13 us (2%)
  matrix products  11.2 us (2%)
  other arithmetic  9.9 us (2%)
    all_gather x2, waiting for transfers between devices, whole_of(): shard = lax.all_gather(shard, axis, axis=dim, tiled=True)  131 us
    all_to_all x1, waiting for transfers between devices, shards(): lax.all_to_all(grad_group, DP, split_axis=1, concat_axis=0, tiled=True)  125 us
    all_gather x1, waiting for transfers between devices, shards(): lax.all_gather(mix, DP, axis=0, tiled=True)  112 us
    all_gather x1, waiting for transfers between devices, shards(): grad_group = lax.all_gather(grad_local, 'mp', axis=0, tiled=True)  83.4 us
    all_to_all x3, starting transfers between devices, from_everyone(): lax.all_to_all(jnp.broadcast_to(shard[None], (count, *shard.shape)), axis...  38 us
    all_to_all x3, waiting for transfers between devices, from_everyone(): lax.all_to_all(jnp.broadcast_to(shard[None], (count, *shard.shape)), axis...  17 us
  transfers between devices with their start and end apart: 8, of which 7 were waited for; matrix products, arithmetic and copies ran while one was open for 4% of the time, Pallas kernels for 0%

commit v1 on v0

--- a/solution.py
+++ b/solution.py
@@ -107,7 +107,7 @@
     ).astype(jnp.bfloat16)
     grad_every = lax.all_to_all(grad_group, DP, split_axis=1, concat_axis=0, tiled=True)
     grad_w_out = lax.dot_general(
-        lax.all_gather(mix, DP, axis=0, tiled=True),
+        jnp.concatenate(lax.all_to_all(jnp.stack([mix] * lax.axis_size(DP)), DP, 0, 0), axis=0),
         grad_every,
         (((0,), (0,)), ((), ())),
         preferred_element_type=jnp.float32,

time: 564 us -> 592 us (1.050)
  blocking collectives: 0 us -> 97.5 us
  waiting for transfers between devices: 470 us -> 398 us
    all_gather x2, waiting for transfers between devices: 131 us -> 287 us  [whole_of(): shard = lax.all_gather(shard, axis, axis=dim, tiled=True)]
    all_gather x1 -> x0, waiting for transfers between devices: 112 us -> none  [shards(): lax.all_gather(mix, DP, axis=0, tiled=True)]
    all_to_all x1, waiting for transfers between devices: 125 us -> 17.5 us  [shards(): lax.all_to_all(jnp.stack([mix] * lax.axis_size(DP)), DP, 0, 0)]
    all_to_all x0 -> x1, blocking collectives: none -> 97.5 us  [shards(): lax.all_to_all(grad_group, DP, split_axis=1, concat_axis=0, tiled=True)]
    all_gather x1, waiting for transfers between devices: 83.4 us -> 75.8 us  [shards(): grad_group = lax.all_gather(grad_local, 'mp', axis=0, tiled=True)]
  transfers between devices with their start and end apart: 8 -> 7, of which waited for: 7 -> 6; matrix products, arithmetic and copies ran while one was open for 4% -> 3% of each run, Pallas kernels for 0% -> 0%
where the time goes in v1:
time: 592 us; the launch traced here: 591 us
  waiting for transfers between devices  398 us (67%)
  blocking collectives  97.5 us (16%)
  starting transfers between devices  44.4 us (8%)
  between operations  18.3 us (3%)
  local copies, waits for them, and re-layouts  11.7 us (2%)
  matrix products  11 us (2%)
  other arithmetic  10.5 us (2%)
    all_gather x2, waiting for transfers between devices, whole_of(): shard = lax.all_gather(shard, axis, axis=dim, tiled=True)  287 us
    all_to_all x1, blocking collectives, shards(): lax.all_to_all(grad_group, DP, split_axis=1, concat_axis=0, tiled=True)  97.5 us
    all_gather x1, waiting for transfers between devices, shards(): grad_group = lax.all_gather(grad_local, 'mp', axis=0, tiled=True)  75.8 us
    all_to_all x3, starting transfers between devices, from_everyone(): lax.all_to_all(jnp.broadcast_to(shard[None], (count, *shard.shape)), axis...  34.9 us
    all_to_all x1, waiting for transfers between devices, shards(): lax.all_to_all(jnp.stack([mix] * lax.axis_size(DP)), DP, 0, 0)  17.5 us
    all_to_all x3, waiting for transfers between devices, from_everyone(): lax.all_to_all(jnp.broadcast_to(shard[None], (count, *shard.shape)), axis...  16.8 us
  transfers between devices with their start and end apart: 7, of which 6 were waited for; matrix products, arithmetic and copies ran while one was open for 3% of the time, Pallas kernels for 0%

profile of v1, /device:TPU:1, one launch (start us, length us, event | category | flops | bytes accessed | tf_op | source)
XLA Modules:
  0.0 590.9 jit_solution(13725907636530914510)
XLA Ops:
  8.0 0.0 copy-start.3
  8.0 0.0 copy-start.2
  9.3 1.3 convert_reduce_fusion
  10.6 0.7 pad_maximum_fusion.1
  11.3 0.6 broadcast_in_dim.17
  11.9 16.1 %all-to-all-start.1 = ((f32[32,1,9]{2,1,0:T(1,128)}), f32[32,1,9]{2,1,0:T(1,128)S(1)}, u32[]{:S(2)}, u32[]{:S(2)}) async-start(f32[32,1,9]{2,1,0:T(1,128)} %broadcast_in_dim.17), calls=%async_computation.1 | async-start | bytes 32768 | tf_op jit(solution)/shard_map/all_to_all | solution.py:14
  28.0 0.7 fusion.15
  28.7 1.4 reduce_max.9
  30.2 2.4 gather_fusion
  32.6 0.7 fusion.14
  33.3 1.7 exponential_reduce_fusion
  35.0 4.3 all-to-all-done.1
  39.3 0.6 broadcast_in_dim.16
  39.9 12.2 %all-to-all-start = ((f32[16,3,128]{2,1,0:T(4,128)}), f32[16,3,128]{2,1,0:T(4,128)S(1)}, u32[]{:S(2)}, u32[]{:S(2)}) async-start(f32[16,3,128]{2,1,0:T(4,128)} %broadcast_in_dim.16), calls=%async_computation | async-start | bytes 65536 | tf_op jit(solution)/shard_map/all_to_all | solution.py:14
  52.1 0.0 all-gather.4.cloned.1.call-start
  52.2 0.1 reduce_sum.56
  52.2 0.6 slice.121
  52.8 0.7 fusion.11
  54.2 12.5 %all-to-all-done = f32[16,3,128]{2,1,0:T(4,128)S(1)} async-done(((f32[16,3,128]{2,1,0:T(4,128)}), f32[16,3,128]{2,1,0:T(4,128)S(1)}, u32[]{:S(2)}, u32[]{:S(2)}) %all-to-all-start) | async-done | bytes 24608 | tf_op jit(solution)/shard_map/all_to_all | solution.py:14
  67.1 0.0 copy-done.3
  67.1 1.8 multiply_reduce_fusion
  68.9 0.1 dynamic-slice_negate_fusion
  68.9 0.0 copy-done.2
  68.9 0.7 multiply_convert_fusion
  69.7 0.0 all-gather.4.cloned.1.call-update
  70.3 0.6 broadcast_in_dim.18
  71.0 6.6 %all-to-all-start.2 = ((f32[32,1,1]{2,1,0:T(1,128)}), f32[32,1,1]{2,1,0:T(1,128)S(1)}, u32[]{:S(2)}, u32[]{:S(2)}) async-start(f32[32,1,1]{2,1,0:T(1,128)} %broadcast_in_dim.18), calls=%async_computation.2 | async-start | bytes 32768 | tf_op jit(solution)/shard_map/all_to_all | solution.py:14
  77.6 75.8 %all-gather.4.cloned.1.call-done = bf16[128,8192]{1,0:T(8,128)(2,1)} async-done(((bf16[8,8192]{1,0:T(8,128)(2,1)}), bf16[128,8192]{1,0:T(8,128)(2,1)}) %all-gather.4.cloned.1.call-update) | async-done | bytes 2097168 | tf_op jit(solution)/shard_map/all_gather | solution.py:101
  153.3 3.2 copy.34
  156.6 0.0 all-to-all-done.2
  156.6 0.0 copy-start.1
  156.6 97.5 %all_to_all.38 = bf16[128,32,256]{0,2,1:T(8,128)(2,1)} all-to-all(bf16[128,32,256]{0,2,1:T(8,128)(2,1)S(1)} %bitcast.48), channel_id=1, replica_groups=mesh['dp_0'=4,'dp_1'=8,'mp'=16] {'dp_0','dp_1'}, dimensions={1} | all-to-all | bytes 4194304 | tf_op jit(solution)/shard_map/all_to_all | solution.py:108
  254.1 0.0 copy-done.1
  254.1 2.4 stack.2
  256.5 9.4 %all-to-all-start.4 = ((bf16[32,128,512]{2,1,0:T(8,128)(2,1)}), bf16[32,128,512]{2,1,0:T(8,128)(2,1)}, u32[]{:S(2)}, u32[]{:S(2)}) async-start(bf16[32,128,512]{2,1,0:T(8,128)(2,1)} %stack.2), calls=%async_computation.4 | async-start | bytes 8388608 | tf_op jit(solution)/shard_map/all_to_all | solution.py:110
  265.9 0.0 all-gather.6.cloned.1.call-start
  266.0 0.5 all-gather.6.cloned.1.call-update
  266.5 0.0 all-gather.8.cloned.1.call-start
  266.6 197.7 %all-gather.6.cloned.1.call-done = bf16[512,2048]{1,0:T(8,128)(2,1)} async-done(((bf16[512,256]{1,0:T(8,128)(2,1)}), bf16[512,2048]{1,0:T(8,128)(2,1)}) %all-gather.6.cloned.1.call-update) | async-done | bytes 2097168 | tf_op jit(solution)/shard_map/all_gather | solution.py:65
  464.2 0.0 all-gather.8.cloned.1.call-update
  464.3 0.6 reduce_sum.59
  464.9 0.0 copy-start
  464.9 17.5 %all-to-all-done.4 = bf16[32,128,512]{2,1,0:T(8,128)(2,1)} async-done(((bf16[32,128,512]{2,1,0:T(8,128)(2,1)}), bf16[32,128,512]{2,1,0:T(8,128)(2,1)}, u32[]{:S(2)}, u32[]{:S(2)}) %all-to-all-start.4) | async-done | bytes 4194336 | tf_op jit(solution)/shard_map/all_to_all | solution.py:110
  482.4 4.1 fusion.8
  486.4 0.8 copy.35
  487.3 89.3 %all-gather.8.cloned.1.call-done = bf16[512,8192]{1,0:T(8,128)(2,1)} async-done(((bf16[512,2048]{1,0:T(8,128)(2,1)}), bf16[512,8192]{1,0:T(8,128)(2,1)}) %all-gather.8.cloned.1.call-update) | async-done | bytes 8388624 | tf_op jit(solution)/shard_map/all_gather | solution.py:65
  576.5 0.0 copy-done
  576.5 7.0 %convolution_convert_fusion = bf16[128,512]{1,0:T(8,128)(2,1)} fusion(bf16[128,8192]{1,0:T(8,128)(2,1)S(1)} %copy-done, bf16[512,8192]{1,0:T(8,128)(2,1)} %all-gather.8.cloned.1.call-done), kind=kOutput, calls=%fused_computation.7 | convolution fusion | flops 1073807360 | bytes 10616832 | tf_op jit(solution)/shard_map/dot_general | solution.py:102
  (31 shorter events, 0.4 us)
Async XLA Ops:
  8.0 59.1 %copy-start.3 = (s32[128]{0:T(128)S(1)}, s32[128]{0:T(128)}, u32[]{:S(2)}) copy-start(s32[128]{0:T(128)} %param.10) | copy-start | bytes 1540
  8.0 60.9 %copy-start.2 = (bf16[8,8192]{1,0:T(8,128)(2,1)S(1)}, bf16[8,8192]{1,0:T(8,128)(2,1)}, u32[]{:S(2)}) copy-start(bf16[8,8192]{1,0:T(8,128)(2,1)} %param.13) | copy-start | bytes 393220
  11.9 27.4 %all-to-all-start.1 = ((f32[32,1,9]{2,1,0:T(1,128)}), f32[32,1,9]{2,1,0:T(1,128)S(1)}, u32[]{:S(2)}, u32[]{:S(2)}) async-start(f32[32,1,9]{2,1,0:T(1,128)} %broadcast_in_dim.17), calls=%async_computation.1 | async-start | bytes 32768 | tf_op jit(solution)/shard_map/all_to_all | solution.py:14
  39.9 26.7 %all-to-all-start = ((f32[16,3,128]{2,1,0:T(4,128)}), f32[16,3,128]{2,1,0:T(4,128)S(1)}, u32[]{:S(2)}, u32[]{:S(2)}) async-start(f32[16,3,128]{2,1,0:T(4,128)} %broadcast_in_dim.16), calls=%async_computation | async-start | bytes 65536 | tf_op jit(solution)/shard_map/all_to_all | solution.py:14
  52.1 101.2 %all-gather.4.cloned.1.call-start = ((), (), s32[]{:S(2)}) async-start(), calls=%async_computation.5 | async-start | bytes 2228224 | tf_op jit(solution)/shard_map/all_gather | solution.py:101
  71.0 85.6 %all-to-all-start.2 = ((f32[32,1,1]{2,1,0:T(1,128)}), f32[32,1,1]{2,1,0:T(1,128)S(1)}, u32[]{:S(2)}, u32[]{:S(2)}) async-start(f32[32,1,1]{2,1,0:T(1,128)} %broadcast_in_dim.18), calls=%async_computation.2 | async-start | bytes 32768 | tf_op jit(solution)/shard_map/all_to_all | solution.py:14
  156.6 97.5 %copy-start.1 = (bf16[128,512]{1,0:T(8,128)(2,1)S(1)}, bf16[128,512]{1,0:T(8,128)(2,1)}, u32[]{:S(2)}) copy-start(bf16[128,512]{1,0:T(8,128)(2,1)} %param.14) | copy-start | bytes 393220
  256.5 225.9 %all-to-all-start.4 = ((bf16[32,128,512]{2,1,0:T(8,128)(2,1)}), bf16[32,128,512]{2,1,0:T(8,128)(2,1)}, u32[]{:S(2)}, u32[]{:S(2)}) async-start(bf16[32,128,512]{2,1,0:T(8,128)(2,1)} %stack.2), calls=%async_computation.4 | async-start | bytes 8388608 | tf_op jit(solution)/shard_map/all_to_all | solution.py:110
  265.9 198.3 %all-gather.6.cloned.1.call-start = ((), (), s32[]{:S(2)}) async-start(), calls=%async_computation.6 | async-start | bytes 2359296 | tf_op jit(solution)/shard_map/all_gather | solution.py:65
  266.5 310.0 %all-gather.8.cloned.1.call-start = ((), (), s32[]{:S(2)}) async-start(), calls=%async_computation.7 | async-start | bytes 10485760 | tf_op jit(solution)/shard_map/all_gather | solution.py:65
  464.9 111.6 %copy-start = (bf16[128,8192]{1,0:T(8,128)(2,1)S(1)}, bf16[128,8192]{1,0:T(8,128)(2,1)}, u32[]{:S(2)}) copy-start(bf16[128,8192]{1,0:T(8,128)(2,1)} %all-gather.4.cloned.1.call-done) | copy-start | bytes 6291460
Sparse Core Ops, SparseCore 0:
  69.8 83.4 all-gather.3
Sparse Core Ops, SparseCore 1:
  268.4 195.8 all-gather.5
  466.2 110.3 all-gather.7
